TPU v7x, 128 devices: a whole 4x4x4 slice. The times are simulated.
128 devices in a mesh: gx: 4 (over y_lo, core), gy: 4 (over z), gz: 8 (over y_hi, x).
Axes of the slice: x: 4, y: 4 (y_hi: 2, y_lo: 2; y = y_hi * 2 + y_lo), z: 4, core: 2. Of those that a mesh axis runs over, the one named last changes fastest.
Arguments:
- source: float32 [256, 256, 256], P('gx', 'gy', 'gz'), may hold values from -6 to 6
- green: float32 [512, 512, 512], P(None, ('gx', 'gz'), 'gy'), may hold values from 0.05 to 2, as said below
Outputs:
- potential: float32 [256, 256, 256], P('gx', 'gy', 'gz')
Inputs may be any that keep to these rules, and one draw needn't show every extreme that they name: `green`: greenfull is even: greenfull[k] equals greenfull at (-k1 mod 512, -k2 mod 512, -k3 mod 512).
All inputs are finite; a program needn't handle non-finite values.
Results may differ from a plain program's by a relative error of at most 0.00007.
Values sent between devices are 32-bit elements; how exact they have to be, the bound alone decides.
A program may use at most 128 MiB of HBM per device.

v0:
```python
import functools

import jax
import jax.numpy as jnp
import numpy as np
from jax import lax
from jax.experimental import pallas as pl
from jax.experimental.pallas import tpu as pltpu
from jax.sharding import PartitionSpec as P

MESH = pl.DeviceIdType.MESH
F32 = jnp.float32
BF16 = jnp.bfloat16
GX, GY, GZ = 4, 4, 8
GROUP = GY * GZ
ALL = GX * GROUP


def halves(table):
    high = np.asarray(table, np.float32).astype(BF16)
    low = (np.asarray(table) - high.astype(np.float64)).astype(np.float32).astype(BF16)
    return np.stack([high, low])


def tables():
    n = np.arange(256)
    angle = 2.0 * np.pi * ((n[:, None] * n[None, :]) % 512) / 512.0
    parity = 1.0 - 2.0 * (n % 2)
    cos, sin = np.cos(angle), np.sin(angle)
    sin_rows = sin.copy()
    sin_rows[0, :] = parity
    sin_cols = sin.copy()
    sin_cols[:, 0] = parity
    lines = np.concatenate([halves(cos), halves(sin_rows), halves(sin_cols)])
    real = cos.reshape(256, 4, 1, 64)
    imag = -sin
    imag[:, 0] = parity
    forward = np.concatenate([real, imag.reshape(256, 4, 1, 64)], axis=2)
    weight = np.full((4, 2, 64), 2.0)
    weight[0, :, 0] = 1.0
    inverse = (forward * weight[None]).reshape(256, 512).T
    return lines, halves(forward.reshape(256, 512)), halves(inverse)


def split(value):
    high = value.astype(BF16)
    return high, (value - high.astype(F32)).astype(BF16)


def dot(left, right):
    return jnp.dot(left, right, preferred_element_type=F32)


def dot3(left, right):
    return dot(left[0], right[0]) + (dot(left[1], right[0]) + dot(left[0], right[1]))


def kernel(src_hbm, green_hbm, lines_hbm, zf_hbm, zi_hbm, out_ref,
           src, lines, zf, zi, got1, zs, zb, snd, rcv, back, gbuf, gs, gmix, snd4, got4,
           in_sem, tab_sem, green_sem, s1, r1, s2, r2, s3, r3, s4, r4):
    a, b, c = lax.axis_index("gx"), lax.axis_index("gy"), lax.axis_index("gz")
    q = b * GZ + c
    me = a * GROUP + q

    load_src = pltpu.make_async_copy(src_hbm, src, in_sem)
    load_src.start()
    loads = [pltpu.make_async_copy(lines_hbm, lines, tab_sem.at[0]),
             pltpu.make_async_copy(zf_hbm, zf, tab_sem.at[1]),
             pltpu.make_async_copy(zi_hbm, zi, tab_sem.at[2])]
    for load in loads:
        load.start()

    def group_peer(o):
        pb = lax.rem(b + o // GZ, GY)
        pc = lax.rem(c + lax.rem(o, GZ), GZ)
        return pb, pc

    def any_peer(o):
        pa = lax.rem(a + o // GROUP, GX)
        pb, pc = group_peer(lax.rem(o, GROUP))
        return pa, pb, pc

    bar = pltpu.get_barrier_semaphore()

    def greet(o, carry):
        pa, pb, pc = any_peer(o)
        pl.semaphore_signal(bar, inc=1, device_id=(pa, pb, pc), device_id_type=MESH)
        return carry

    lax.fori_loop(1, ALL, greet, 0)
    pl.semaphore_wait(bar, ALL - 1)
    load_src.wait()

    def send1(o, carry):
        pb, pc = group_peer(o)
        pltpu.make_async_remote_copy(
            src.at[pb * GZ + pc], got1.at[q], s1, r1, device_id=(a, pb, pc), device_id_type=MESH
        ).start()
        return carry

    lax.fori_loop(1, GROUP, send1, 0)
    got1[q] = src[q]

    pltpu.make_async_copy(green_hbm.at[pl.ds(0, 257)], gbuf.at[pl.ds(0, 257)], green_sem).start()

    def load_green(k, carry):
        pltpu.make_async_copy(green_hbm.at[512 - k], gbuf.at[256 + k], green_sem).start()
        return carry

    lax.fori_loop(1, 256, load_green, 0)
    for load in loads:
        load.wait()
    def wait_bytes(part, sem):
        pltpu.make_async_copy(part, part, sem).wait()

    wait_bytes(got1.at[pl.ds(0, GROUP - 1)], r1)

    lane = lax.broadcasted_iota(jnp.int32, (16, 128), 1) // 32

    for i in range(2):
        def gather(t, carry):
            tb, th = t // 2, lax.rem(t, 2)
            pieces = [got1[tb * GZ + th * 4 + m, i] for m in range(4)]
            for yh in range(4):
                tile = pieces[0] if yh == 0 else pltpu.roll(pieces[0], (-yh * 32) % 128, 1)
                for m in range(1, 4):
                    shift = ((m - yh) * 32) % 128
                    moved = pieces[m] if shift == 0 else pltpu.roll(pieces[m], shift, 1)
                    tile = jnp.where(lane == m, moved, tile)
                row = pl.multiple_of(tb * 64 + yh * 16, 16)
                zs[th, i, pl.ds(row, 16), :] = tile
            return carry

        lax.fori_loop(0, 8, gather, 0)

    sign = jnp.where(lax.broadcasted_iota(jnp.int32, (1, 128), 1) < 64, 1.0, -1.0).astype(F32)
    real_lane = lax.broadcasted_iota(jnp.int32, (1, 128), 1) == 0
    imag_lane = lax.broadcasted_iota(jnp.int32, (1, 128), 1) == 64
    unit_lane = jnp.logical_or(real_lane, imag_lane)
    top_row = lax.broadcasted_iota(jnp.int32, (8, 1), 0) == 0

    def turn(value):
        return sign * pltpu.roll(value, 64, 1)

    def fix_top(value, top):
        return jnp.concatenate([jnp.where(top_row, top, value[:8]), value[8:]], axis=0)

    cos = (lines[0], lines[1])
    sin_rows = (lines[2], lines[3])
    sin_cols = (lines[4], lines[5])

    for i in range(2):
        rows = jnp.concatenate([zs[0, i], zs[1, i]], axis=1)
        zb[i] = dot3(split(rows), (zf[0], zf[1]))

    snd_view = snd.reshape(2, GX, GY, GZ, 2, 8, 128)

    def forward_y(t, carry):
        i, tb = t // GY, lax.rem(t, GY)
        column = pl.multiple_of(tb * 128, 128)
        value = zb[i, :, pl.ds(column, 128)]
        even = dot3(cos, split(value))
        odd = dot3(sin_rows, split(turn(value)))
        plus, minus = even + odd, even - odd
        special = jnp.logical_and(unit_lane, tb == 0)
        even_turn, odd_turn = pltpu.roll(even, 64, 1), pltpu.roll(odd, 64, 1)
        plus = jnp.where(special, jnp.where(real_lane, even, odd), plus)
        minus = jnp.where(special, jnp.where(real_lane, even_turn, -odd_turn), minus)
        plus = fix_top(plus, even[:8])
        minus = fix_top(minus, -sign * odd_turn[:8])
        snd_view[0, :, tb, :, i] = plus.reshape(GX, GZ, 8, 128)
        snd_view[1, :, tb, :, i] = minus.reshape(GX, GZ, 8, 128)
        return carry

    lax.fori_loop(0, 2 * GY, forward_y, 0)

    for s in range(2):
        def send2(o, carry):
            pa, pb, pc = any_peer(o)
            pltpu.make_async_remote_copy(
                snd.at[s, pa * GROUP + pb * GZ + pc], rcv.at[s, pl.ds(2 * me, 2)], s2.at[s], r2.at[s],
                device_id=(pa, pb, pc), device_id_type=MESH
            ).start()
            return carry

        lax.fori_loop(1, ALL, send2, 0)
        rcv[s, pl.ds(2 * me, 2)] = snd[s, me]

    pltpu.make_async_copy(green_hbm, gbuf, green_sem).wait()
    green_rows = gbuf.reshape(512 * 16, 128)
    corner = jnp.logical_and(b == 0, jnp.logical_and(a == 0, c == 0))
    pick = 2 * lax.rem(lax.broadcasted_iota(jnp.int32, (512, 128), 1), 64)

    def prepare(jj, carry):
        first = green_rows[pl.ds(2 * jj, 512, stride=16), :]
        second = green_rows[pl.ds(2 * jj + 1, 512, stride=16), :]
        here = jnp.logical_and(corner, jj == 0)
        plus = jnp.take_along_axis(first, pick, axis=1)
        minus = jnp.take_along_axis(second, pick, axis=1)
        first0, first1 = first[:, 0:1], first[:, 1:2]
        second0, second1 = second[:, 0:1], second[:, 1:2]
        at_unit = jnp.logical_and(unit_lane, b == 0)
        plus_unit = jnp.where(here, 0.5 * (first0 + first1), first0)
        minus_unit = jnp.where(here, 0.5 * (second0 + second1), first1)
        gs[0, jj] = jnp.where(at_unit, plus_unit, plus)
        gs[1, jj] = jnp.where(at_unit, minus_unit, minus)

        @pl.when(jj == 0)
        def _():
            gmix[0] = jnp.where(jnp.logical_and(unit_lane, here), 0.5 * (first0 - first1), 0.0)
            gmix[1] = jnp.where(jnp.logical_and(unit_lane, here), 0.5 * (second0 - second1), 0.0)

        return carry

    lax.fori_loop(0, 8, prepare, 0)

    def wide(left, right):
        return jnp.concatenate([left, right], axis=1)

    rcv_rows = rcv.reshape(2 * 256 * 8, 128)
    for s in range(2):
        wait_bytes(rcv.at[s, pl.ds(0, 2 * (ALL - 1))], r2.at[s])

        def lines_x(jp, carry):
            first = pl.ds(s * 2048 + 2 * jp, 256, stride=8)
            second = pl.ds(s * 2048 + 2 * jp + 1, 256, stride=8)
            left, right = rcv_rows[first, :], rcv_rows[second, :]
            even = dot3(cos, split(wide(left, right)))
            odd = dot3(sin_rows, split(wide(turn(left), turn(right))))
            results = []
            for h in range(2):
                ev, od = even[:, h * 128:(h + 1) * 128], odd[:, h * 128:(h + 1) * 128]
                plus = fix_top(ev + od, ev[:8])
                minus = fix_top(ev - od, -turn(od[:8]))
                out_plus = plus * gs[s, 2 * jp + h, 0:256]
                out_minus = minus * gs[s, 2 * jp + h, 256:512]
                if h == 0:
                    mix = jnp.where(jp == 0, 1.0, 0.0) * sign
                    out_plus += gmix[s, 0:256] * (mix * fix_top(minus, plus[:8]))
                    out_minus += gmix[s, 256:512] * (mix * fix_top(plus, minus[:8]))
                total = fix_top(out_plus + out_minus, out_plus[:8])
                turned = fix_top(turn(out_plus - out_minus), -out_minus[:8])
                results.append((total, turned))
            total = wide(results[0][0], results[1][0])
            turned = wide(results[0][1], results[1][1])
            back_x = dot3(cos, split(total)) - dot3(sin_cols, split(turned))
            rcv_rows[first, :] = back_x[:, :128]
            rcv_rows[second, :] = back_x[:, 128:]
            return carry

        lax.fori_loop(0, 4, lines_x, 0)

        def send3(o, carry):
            pa, pb, pc = any_peer(o)
            peer = pa * GROUP + pb * GZ + pc
            pltpu.make_async_remote_copy(
                rcv.at[s, pl.ds(2 * peer, 2)], back.at[s, me], s3.at[s], r3.at[s],
                device_id=(pa, pb, pc), device_id_type=MESH
            ).start()
            return carry

        lax.fori_loop(1, ALL, send3, 0)
        back[s, me] = rcv[s, pl.ds(2 * me, 2)]

    for s in range(2):
        wait_bytes(back.at[s, pl.ds(0, ALL - 1)], r3.at[s])

    back_view = back.reshape(2, GX, GY, GZ, 2, 8, 128)

    def inverse_y(t, carry):
        i, tb = t // GY, lax.rem(t, GY)
        plus = back_view[0, :, tb, :, i].reshape(256, 128)
        minus = back_view[1, :, tb, :, i].reshape(256, 128)
        special = jnp.logical_and(unit_lane, tb == 0)
        total = plus + minus
        turned = turn(plus - minus)
        total = jnp.where(special, 2.0 * jnp.where(real_lane, plus, pltpu.roll(minus, 64, 1)), total)
        turned = jnp.where(special, 2.0 * jnp.where(real_lane, pltpu.roll(plus, 64, 1), minus), turned)
        total = fix_top(total, plus[:8])
        turned = fix_top(turned, -minus[:8])
        column = pl.multiple_of(tb * 128, 128)
        zb[i, :, pl.ds(column, 128)] = dot3(cos, split(total)) - dot3(sin_cols, split(turned))
        return carry

    lax.fori_loop(0, 2 * GY, inverse_y, 0)

    for i in range(2):
        rows = dot3(split(zb[i]), (zi[0], zi[1])) * (1.0 / 134217728.0)
        zs[0, i] = rows[:, :128]
        zs[1, i] = rows[:, 128:]

    for i in range(2):
        def scatter(t, carry):
            tb, th = t // 2, lax.rem(t, 2)
            pieces = []
            for yh in range(4):
                row = pl.multiple_of(tb * 64 + yh * 16, 16)
                pieces.append(zs[th, i, pl.ds(row, 16), :])
            for m in range(4):
                tile = pieces[0] if m == 0 else pltpu.roll(pieces[0], (-m * 32) % 128, 1)
                for yh in range(1, 4):
                    shift = ((yh - m) * 32) % 128
                    moved = pieces[yh] if shift == 0 else pltpu.roll(pieces[yh], shift, 1)
                    tile = jnp.where(lane == yh, moved, tile)
                snd4[tb * GZ + th * 4 + m, i] = tile
            return carry

        lax.fori_loop(0, 8, scatter, 0)

    def send4(o, carry):
        pb, pc = group_peer(o)
        pltpu.make_async_remote_copy(
            snd4.at[pb * GZ + pc], got4.at[q], s4, r4, device_id=(a, pb, pc), device_id_type=MESH
        ).start()
        return carry

    lax.fori_loop(1, GROUP, send4, 0)
    got4[q] = snd4[q]
    for s in range(2):
        wait_bytes(snd.at[s, pl.ds(0, ALL - 1)], s2.at[s])
        wait_bytes(rcv.at[s, pl.ds(0, 2 * (ALL - 1))], s3.at[s])
    for ref, sem in ((src, s1), (got4, r4), (snd4, s4)):
        wait_bytes(ref.at[pl.ds(0, GROUP - 1)], sem)
    out_ref[...] = got4[...]


def per_device(source, green):
    lines, forward, inverse = tables()
    packed = source.reshape(64, 4, 16, 32).transpose(0, 2, 1, 3).reshape(GROUP, 2, 16, 128)
    vmem = pltpu.VMEM
    dma = pltpu.SemaphoreType.DMA
    result = pl.pallas_call(
        kernel,
        out_shape=jax.ShapeDtypeStruct((GROUP, 2, 16, 128), F32),
        in_specs=[pl.BlockSpec(memory_space=pl.ANY)] * 5,
        out_specs=pl.BlockSpec(memory_space=vmem),
        scratch_shapes=[
            vmem((GROUP, 2, 16, 128), F32),
            vmem((6, 256, 256), BF16),
            vmem((2, 256, 512), BF16),
            vmem((2, 512, 256), BF16),
            vmem((GROUP, 2, 16, 128), F32),
            vmem((2, 2, 256, 128), F32),
            vmem((2, 256, 512), F32),
            vmem((2, ALL, 2, 8, 128), F32),
            vmem((2, 256, 8, 128), F32),
            vmem((2, ALL, 2, 8, 128), F32),
            vmem((512, 16, 128), F32),
            vmem((2, 8, 512, 128), F32),
            vmem((2, 512, 128), F32),
            vmem((GROUP, 2, 16, 128), F32),
            vmem((GROUP, 2, 16, 128), F32),
            dma, dma((3,)), dma, dma, dma, dma((2,)), dma((2,)), dma((2,)), dma((2,)), dma, dma,
        ],
        compiler_params=pltpu.CompilerParams(
            collective_id=1, has_side_effects=True, vmem_limit_bytes=56 * 2**20
        ),
        name="poisson",
    )(packed, green, jnp.asarray(lines), jnp.asarray(forward), jnp.asarray(inverse))
    return result.reshape(64, 16, 4, 32).transpose(0, 2, 1, 3).reshape(64, 64, 32)


def solution(mesh):
    return jax.shard_map(
        per_device,
        mesh=mesh,
        in_specs=(P("gx", "gy", "gz"), P(None, ("gx", "gz"), "gy")),
        out_specs=P("gx", "gy", "gz"),
        check_vma=False,
    )
```

profile of v0, /device:TPU:0, one launch (start us, length us, event | category | flops | bytes accessed | tf_op | source)
XLA Modules:
  0.0 103.8 jit_solution(6580384348261289793)
XLA Ops:
  0.0 2.2 %copy.8 = f32[64,64,32]{0,2,1:T(8,128)S(1)} copy(f32[64,64,32]{1,2,0:T(8,128)} %param.5) | data formatting | bytes 1048576 | tf_op args[0]
  2.3 2.4 %copy.9 = f32[64,16,4,32]{3,2,1,0:T(4,128)S(1)} copy(f32[64,16,4,32]{0,3,1,2:T(8,128)S(1)} %bitcast.9) | data formatting | bytes 1048576 | tf_op jit(solution)/shard_map/transpose | solution.py:329
  4.6 1.7 %reshape.13.src_hbm = f32[32,2,16,128]{3,2,1,0:T(8,128)} reshape(f32[64,16,4,32]{3,2,1,0:T(4,128)S(1)} %copy.9) | data formatting | bytes 1048576 | tf_op jit(solution)/shard_map/reshape | solution.py:329
  6.3 92.2 %poisson.1 = f32[32,2,16,128]{3,2,1,0:T(8,128)} custom-call(f32[32,2,16,128]{3,2,1,0:T(8,128)} %reshape.13.src_hbm, f32[512,16,128]{2,1,0:T(8,128)} %green_hbm.1, bf16[6,256,256]{2,1,0:T(8,128)(2,1)} %constant.6.clone.lines_hbm, bf16[2,256,512]{2,1,0:T(8,128)(2,1)} %constant.7.clone.zf_hbm, bf16[2,512,256]{2,1,0:T(8,128)(2,1)} %constant.8.clone.zi_hbm), custom_call_target="tpu_custom_call" | custom-call | tf_op jit(solution)/shard_map/poisson/pallas_call | solution.py:332
  98.5 2.1 %reshape.14 = f32[64,16,4,32]{3,2,1,0:T(4,128)S(1)} reshape(f32[32,2,16,128]{3,2,1,0:T(8,128)} %poisson.1) | data formatting | bytes 1048576 | tf_op jit(solution)/shard_map/reshape | solution.py:360
  100.6 1.2 %copy.10 = f32[64,4,16,32]{0,3,2,1:T(8,128)S(1)} copy(f32[64,4,16,32]{3,1,2,0:T(4,128)S(1)} %bitcast.7) | data formatting | bytes 1048576 | tf_op jit(solution)/shard_map/transpose | solution.py:360
  101.9 2.0 %copy.11 = f32[64,64,32]{1,2,0:T(8,128)} copy(f32[64,64,32]{0,2,1:T(8,128)S(1)} %bitcast.8) | data formatting | bytes 1048576 | tf_op jit(solution)/shard_map/reshape | solution.py:360
where the time goes:
time: 104 us
  Pallas kernels  92.2 us (89%)
  local copies, waits for them, and re-layouts  11.6 us (11%)
    pallas_call x1, Pallas kernels, per_device(): pl.pallas_call(kernel, out_shape=jax.ShapeDtypeStruct((GROUP, 2, 16, 128)...  92.2 us
    reshape x2, local copies, waits for them, and re-layouts, per_device(): result.reshape(64, 16, 4, 32).transpose(0, 2, 1, 3).reshape(64, 64, 32)  4.06 us
    transpose x1, local copies, waits for them, and re-layouts, per_device(): source.reshape(64, 4, 16, 32).transpose(0, 2, 1, 3)  2.36 us
    unnamed x1, local copies, waits for them, and re-layouts  2.24 us

commit v1 on v0

v1 whole, which is shorter than its diff:
```python
import jax
import jax.numpy as jnp
import numpy as np
from jax import lax
from jax.experimental import pallas as pl
from jax.experimental.pallas import tpu as pltpu
from jax.sharding import PartitionSpec as P

FLAT = pl.DeviceIdType.LOGICAL
F32 = jnp.float32
BF16 = jnp.bfloat16
GX, GY, GZ = 4, 4, 8
GROUP = GY * GZ
ALL = GX * GROUP


def halves(table):
    high = np.asarray(table, np.float32).astype(BF16)
    low = (np.asarray(table) - high.astype(np.float64)).astype(np.float32).astype(BF16)
    return np.stack([high, low])


def tables():
    n = np.arange(256)
    angle = 2.0 * np.pi * ((n[:, None] * n[None, :]) % 512) / 512.0
    parity = 1.0 - 2.0 * (n % 2)
    cos, sin = np.cos(angle), np.sin(angle)
    sin_rows = sin.copy()
    sin_rows[0, :] = parity
    sin_cols = sin.copy()
    sin_cols[:, 0] = parity
    lines = np.concatenate([halves(cos), halves(sin_rows), halves(sin_cols)])
    real = cos.reshape(256, 4, 1, 64)
    imag = -sin
    imag[:, 0] = parity
    forward = np.concatenate([real, imag.reshape(256, 4, 1, 64)], axis=2)
    weight = np.full((4, 2, 64), 2.0)
    weight[0, :, 0] = 1.0
    inverse = (forward * weight[None]).reshape(256, 512)
    return lines, halves(forward.reshape(256, 512)), halves(inverse)


def split(value):
    high = value.astype(BF16)
    return high, (value - high.astype(F32)).astype(BF16)


def dot(left, right):
    return jnp.dot(left, right, preferred_element_type=F32)


def dot_t(left, right):
    return lax.dot_general(left, right, (((1,), (1,)), ((), ())), preferred_element_type=F32)


def dot3(left, right):
    return dot(left[0], right[0]) + (dot(left[1], right[0]) + dot(left[0], right[1]))


def wide(left, right):
    return jnp.concatenate([left, right], axis=1)


def kernel(src_hbm, green_hbm, lines_hbm, zf_hbm, zi_hbm, out_ref,
           src, pack, lines, zf, zi, got1, zs, zb, snd, rcv, back0, back1, gbuf, gs, gmix, snd4, got4,
           in_sem, tab_sem, green_sem, s1, r1, s2, r2, s30, r30, s31, r31, s4, r4):
    a, b, c = lax.axis_index("gx"), lax.axis_index("gy"), lax.axis_index("gz")
    q = b * GZ + c
    me = a * GROUP + q

    load_src = pltpu.make_async_copy(src_hbm, src, in_sem)
    load_src.start()
    loads = [pltpu.make_async_copy(lines_hbm, lines, tab_sem.at[0]),
             pltpu.make_async_copy(zf_hbm, zf, tab_sem.at[1]),
             pltpu.make_async_copy(zi_hbm, zi, tab_sem.at[2])]
    for load in loads:
        load.start()

    def wait_bytes(part, sem):
        pltpu.make_async_copy(part, part, sem).wait()

    def each_peer(count, body):
        def step(o, carry):
            body(lax.bitwise_xor(me, o))
            return carry

        lax.fori_loop(1, count, step, 0, unroll=8)

    bar = pltpu.get_barrier_semaphore()

    def greet(peer):
        pl.semaphore_signal(bar, inc=1, device_id=peer, device_id_type=FLAT)

    each_peer(GROUP, greet)
    for o in range(1, GX):
        greet(lax.bitwise_xor(me, o * GROUP))
    load_src.wait()

    def pack_x(p, carry):
        for i in range(2):
            plane = src[2 * p + i]
            pack[i, p] = wide(plane[:16], plane[16:])
        return carry

    lax.fori_loop(0, GROUP, pack_x, 0, unroll=4)
    pl.semaphore_wait(bar, GROUP - 1 + GX - 1)

    for i in range(2):
        def send1(peer):
            pltpu.make_async_remote_copy(
                pack.at[i, lax.rem(peer, GROUP)], got1.at[i, q], s1.at[i], r1.at[i],
                device_id=peer, device_id_type=FLAT
            ).start()

        each_peer(GROUP, send1)
        got1[i, q] = pack[i, q]

    pltpu.make_async_copy(green_hbm.at[pl.ds(0, 257)], gbuf.at[pl.ds(0, 257)], green_sem).start()

    def load_green(k, carry):
        pltpu.make_async_copy(green_hbm.at[512 - k], gbuf.at[256 + k], green_sem).start()
        return carry

    lax.fori_loop(1, 256, load_green, 0, unroll=5)
    for load in loads:
        load.wait()

    low_lane = lax.broadcasted_iota(jnp.int32, (1, 128), 1) < 64
    sign = jnp.where(low_lane, 1.0, -1.0).astype(F32)
    real_lane = lax.broadcasted_iota(jnp.int32, (1, 128), 1) == 0
    imag_lane = lax.broadcasted_iota(jnp.int32, (1, 128), 1) == 64
    unit_lane = jnp.logical_or(real_lane, imag_lane)
    top_row = lax.broadcasted_iota(jnp.int32, (8, 1), 0) == 0

    def half_turn(value):
        return pltpu.roll(value, 64, 1)

    def turn(value):
        return sign * half_turn(value)

    def fix_top(value, top):
        return jnp.concatenate([jnp.where(top_row, top, value[:8]), value[8:]], axis=0)

    cos = (lines[0], lines[1])
    sin_rows = (lines[2], lines[3])
    sin_cols = (lines[4], lines[5])
    snd_view = snd.reshape(2, 2, GX, GY, GZ, 8, 128)

    def send2(s, i):
        def send(peer):
            pltpu.make_async_remote_copy(
                snd.at[s, i, peer], rcv.at[s, 2 * me + i], s2.at[s], r2.at[s],
                device_id=peer, device_id_type=FLAT
            ).start()

        each_peer(ALL, send)
        rcv[s, 2 * me + i] = snd[s, i, me]

    for i in range(2):
        wait_bytes(got1.at[i, pl.ds(0, GROUP - 1)], r1.at[i])

        def gather(t, carry):
            for th in range(2):
                left = got1[i, 2 * th * GZ + t]
                right = got1[i, (2 * th + 1) * GZ + t]
                row = pl.multiple_of(t * 32, 32)
                zs[pl.ds(row, 16), th * 128:(th + 1) * 128] = jnp.where(low_lane, left, half_turn(right))
                zs[pl.ds(row + 16, 16), th * 128:(th + 1) * 128] = jnp.where(low_lane, half_turn(left), right)
            return carry

        lax.fori_loop(0, GZ, gather, 0, unroll=2)
        zb[...] = dot3(split(jnp.transpose(zs[...])), (zf[0], zf[1]))

        def forward_y(t, carry):
            column = pl.multiple_of(t * 256, 256)
            value = zb[:, pl.ds(column, 256)]
            even = dot3(cos, split(value))
            odd = dot3(sin_rows, split(wide(turn(value[:, :128]), turn(value[:, 128:]))))
            for h in range(2):
                ev, od = even[:, h * 128:(h + 1) * 128], odd[:, h * 128:(h + 1) * 128]
                plus, minus = ev + od, ev - od
                if h == 0:
                    special = jnp.logical_and(unit_lane, t == 0)
                    plus = jnp.where(special, jnp.where(real_lane, ev, od), plus)
                    minus = jnp.where(special, jnp.where(real_lane, half_turn(ev), -half_turn(od)), minus)
                plus = fix_top(plus, ev[:8])
                minus = fix_top(minus, -turn(od[:8]))
                snd_view[0, i, :, 2 * t + h] = plus.reshape(GX, GZ, 8, 128)
                snd_view[1, i, :, 2 * t + h] = minus.reshape(GX, GZ, 8, 128)
            return carry

        lax.fori_loop(0, GY // 2, forward_y, 0)
        send2(0, i)
    for i in range(2):
        send2(1, i)

    pltpu.make_async_copy(green_hbm, gbuf, green_sem).wait()
    green_rows = gbuf.reshape(512 * 16, 128)
    corner = jnp.logical_and(b == 0, jnp.logical_and(a == 0, c == 0))
    pick = 2 * lax.rem(lax.broadcasted_iota(jnp.int32, (512, 128), 1), 64)

    def prepare(jj, carry):
        first = green_rows[pl.ds(2 * jj, 512, stride=16), :]
        second = green_rows[pl.ds(2 * jj + 1, 512, stride=16), :]
        here = jnp.logical_and(corner, jj == 0)
        plus = jnp.take_along_axis(first, pick, axis=1)
        minus = jnp.take_along_axis(second, pick, axis=1)
        first0, first1 = first[:, 0:1], first[:, 1:2]
        second0, second1 = second[:, 0:1], second[:, 1:2]
        at_unit = jnp.logical_and(unit_lane, b == 0)
        plus_unit = jnp.where(here, 0.5 * (first0 + first1), first0)
        minus_unit = jnp.where(here, 0.5 * (second0 + second1), first1)
        gs[0, jj] = jnp.where(at_unit, plus_unit, plus)
        gs[1, jj] = jnp.where(at_unit, minus_unit, minus)

        @pl.when(jj == 0)
        def _():
            gmix[0] = jnp.where(jnp.logical_and(unit_lane, here), 0.5 * (first0 - first1), 0.0)
            gmix[1] = jnp.where(jnp.logical_and(unit_lane, here), 0.5 * (second0 - second1), 0.0)

        return carry

    lax.fori_loop(0, 8, prepare, 0)

    rcv_rows = rcv.reshape(2 * 256 * 8, 128)
    for s in range(2):
        wait_bytes(rcv.at[s, pl.ds(0, 2 * (ALL - 1))], r2.at[s])

        def lines_x(jp, carry):
            first = pl.ds(s * 2048 + 2 * jp, 256, stride=8)
            second = pl.ds(s * 2048 + 2 * jp + 1, 256, stride=8)
            left, right = rcv_rows[first, :], rcv_rows[second, :]
            even = dot3(cos, split(wide(left, right)))
            odd = dot3(sin_rows, split(wide(turn(left), turn(right))))
            results = []
            for h in range(2):
                ev, od = even[:, h * 128:(h + 1) * 128], odd[:, h * 128:(h + 1) * 128]
                plus = fix_top(ev + od, ev[:8])
                minus = fix_top(ev - od, -turn(od[:8]))
                out_plus = plus * gs[s, 2 * jp + h, 0:256]
                out_minus = minus * gs[s, 2 * jp + h, 256:512]
                if h == 0:
                    mix = jnp.where(jp == 0, 1.0, 0.0) * sign
                    out_plus += gmix[s, 0:256] * (mix * fix_top(minus, plus[:8]))
                    out_minus += gmix[s, 256:512] * (mix * fix_top(plus, minus[:8]))
                total = fix_top(out_plus + out_minus, out_plus[:8])
                turned = fix_top(turn(out_plus - out_minus), -out_minus[:8])
                results.append((total, turned))
            total = wide(results[0][0], results[1][0])
            turned = wide(results[0][1], results[1][1])
            back_x = dot3(cos, split(total)) - dot3(sin_cols, split(turned))
            rcv_rows[first, :] = back_x[:, :128]
            rcv_rows[second, :] = back_x[:, 128:]
            return carry

        lax.fori_loop(0, 4, lines_x, 0)

        if s == 0:
            def send30(peer):
                pltpu.make_async_remote_copy(
                    rcv.at[0, pl.ds(2 * peer, 2)], back0.at[me], s30, r30,
                    device_id=peer, device_id_type=FLAT
                ).start()

            each_peer(ALL, send30)
            back0[me] = rcv[0, pl.ds(2 * me, 2)]
        else:
            for i in range(2):
                def send31(peer):
                    pltpu.make_async_remote_copy(
                        rcv.at[1, 2 * peer + i], back1.at[i, me], s31.at[i], r31.at[i],
                        device_id=peer, device_id_type=FLAT
                    ).start()

                each_peer(ALL, send31)
                back1[i, me] = rcv[1, 2 * me + i]

    back0_view = back0.reshape(GX, GY, GZ, 2, 8, 128)
    back1_view = back1.reshape(2, GX, GY, GZ, 8, 128)
    wait_bytes(back0.at[pl.ds(0, ALL - 1)], r30)
    for i in range(2):
        wait_bytes(back1.at[i, pl.ds(0, ALL - 1)], r31.at[i])

        def inverse_y(t, carry):
            totals, turneds = [], []
            for h in range(2):
                plus = back0_view[:, 2 * t + h, :, i].reshape(256, 128)
                minus = back1_view[i, :, 2 * t + h].reshape(256, 128)
                total = plus + minus
                turned = turn(plus - minus)
                if h == 0:
                    special = jnp.logical_and(unit_lane, t == 0)
                    total = jnp.where(special, 2.0 * jnp.where(real_lane, plus, half_turn(minus)), total)
                    turned = jnp.where(special, 2.0 * jnp.where(real_lane, half_turn(plus), minus), turned)
                totals.append(fix_top(total, plus[:8]))
                turneds.append(fix_top(turned, -minus[:8]))
            column = pl.multiple_of(t * 256, 256)
            zb[:, pl.ds(column, 256)] = (
                dot3(cos, split(wide(*totals))) - dot3(sin_cols, split(wide(*turneds)))
            )
            return carry

        lax.fori_loop(0, GY // 2, inverse_y, 0)
        high, low = split(zb[...])
        zs[...] = (dot_t(zi[0], high) + (dot_t(zi[1], high) + dot_t(zi[0], low))) * (1.0 / 134217728.0)

        def scatter(t, carry):
            row = pl.multiple_of(t * 32, 32)
            for th in range(2):
                upper = zs[pl.ds(row, 16), th * 128:(th + 1) * 128]
                lower = zs[pl.ds(row + 16, 16), th * 128:(th + 1) * 128]
                snd4[i, 2 * th * GZ + t] = jnp.where(low_lane, upper, half_turn(lower))
                snd4[i, (2 * th + 1) * GZ + t] = jnp.where(low_lane, half_turn(upper), lower)
            return carry

        lax.fori_loop(0, GZ, scatter, 0, unroll=2)

        def send4(peer):
            pltpu.make_async_remote_copy(
                snd4.at[i, lax.rem(peer, GROUP)], got4.at[i, q], s4.at[i], r4.at[i],
                device_id=peer, device_id_type=FLAT
            ).start()

        each_peer(GROUP, send4)
        got4[i, q] = snd4[i, q]

    for s in range(2):
        wait_bytes(pack.at[s, pl.ds(0, GROUP - 1)], s1.at[s])
        wait_bytes(rcv.at[s, pl.ds(0, 2 * (ALL - 1))], s2.at[s])
        wait_bytes(back1.at[s, pl.ds(0, ALL - 1)], s31.at[s])
    wait_bytes(back0.at[pl.ds(0, ALL - 1)], s30)
    for i in range(2):
        wait_bytes(got4.at[i, pl.ds(0, GROUP - 1)], r4.at[i])

        def unpack(p, carry):
            value = got4[i, p]
            out_ref[2 * p + i, 0:16] = value[:, :64]
            out_ref[2 * p + i, 16:32] = value[:, 64:]
            return carry

        lax.fori_loop(0, GROUP, unpack, 0, unroll=4)
    for i in range(2):
        wait_bytes(snd4.at[i, pl.ds(0, GROUP - 1)], s4.at[i])


def per_device(source, green):
    lines, forward, inverse = tables()
    vmem = pltpu.VMEM
    dma = pltpu.SemaphoreType.DMA
    result = pl.pallas_call(
        kernel,
        out_shape=jax.ShapeDtypeStruct((64, 32, 64), F32),
        in_specs=[pl.BlockSpec(memory_space=pl.ANY)] * 5,
        out_specs=pl.BlockSpec(memory_space=vmem),
        scratch_shapes=[
            vmem((64, 32, 64), F32),
            vmem((2, GROUP, 16, 128), F32),
            vmem((6, 256, 256), BF16),
            vmem((2, 256, 512), BF16),
            vmem((2, 256, 512), BF16),
            vmem((2, GROUP, 16, 128), F32),
            vmem((256, 256), F32),
            vmem((256, 512), F32),
            vmem((2, 2, ALL, 8, 128), F32),
            vmem((2, 256, 8, 128), F32),
            vmem((ALL, 2, 8, 128), F32),
            vmem((2, ALL, 8, 128), F32),
            vmem((512, 16, 128), F32),
            vmem((2, 8, 512, 128), F32),
            vmem((2, 512, 128), F32),
            vmem((2, GROUP, 16, 128), F32),
            vmem((2, GROUP, 16, 128), F32),
            dma, dma((3,)), dma, dma((2,)), dma((2,)), dma((2,)), dma((2,)),
            dma, dma, dma((2,)), dma((2,)), dma((2,)), dma((2,)),
        ],
        compiler_params=pltpu.CompilerParams(
            collective_id=1, has_side_effects=True, vmem_limit_bytes=56 * 2**20
        ),
        name="poisson",
    )(jnp.transpose(source, (0, 2, 1)), green,
      jnp.asarray(lines), jnp.asarray(forward), jnp.asarray(inverse))
    return jnp.transpose(result, (0, 2, 1))


def solution(mesh):
    return jax.shard_map(
        per_device,
        mesh=mesh,
        in_specs=(P("gx", "gy", "gz"), P(None, ("gx", "gz"), "gy")),
        out_specs=P("gx", "gy", "gz"),
        check_vma=False,
    )
```

time: 104 us -> 82.7 us (0.80)
  Pallas kernels: 92.2 us -> 80 us
  local copies, waits for them, and re-layouts: 11.6 us -> 2.26 us
    pallas_call x1, Pallas kernels: 92.2 us -> 80 us  [per_device(): pl.pallas_call(kernel, out_shape=jax.ShapeDtypeStruct((64, 32, 64), F32),...]
    reshape x3 -> x0, local copies, waits for them, and re-layouts: 5.73 us -> none  [the longest x2 4.06 us: per_device(): result.reshape(64, 16, 4, 32).transpose(0, 2, 1, 3).reshape(64, 64, 32)]
    transpose x2 -> x0, local copies, waits for them, and re-layouts: 3.59 us -> none  [the longest x1 2.36 us: per_device(): source.reshape(64, 4, 16, 32).transpose(0, 2, 1, 3)]
where the time goes in v1:
time: 82.7 us; the launch traced here: 82.3 us
  Pallas kernels  80 us (97%)
  local copies, waits for them, and re-layouts  2.26 us (3%)
    pallas_call x1, Pallas kernels, per_device(): pl.pallas_call(kernel, out_shape=jax.ShapeDtypeStruct((64, 32, 64), F32),...  80 us
    unnamed x1, local copies, waits for them, and re-layouts  2.26 us

profile of v1, /device:TPU:0, one launch (start us, length us, event | category | flops | bytes accessed | tf_op | source)
XLA Modules:
  0.0 82.3 jit_solution(3058625394214097575)
XLA Ops:
  0.0 80.0 %poisson.1 = f32[64,32,64]{2,1,0:T(8,128)} custom-call(f32[64,32,64]{2,1,0:T(8,128)} %bitcast.3, f32[512,16,128]{2,1,0:T(8,128)} %green_hbm.1, bf16[6,256,256]{2,1,0:T(8,128)(2,1)} %constant.6.clone.lines_hbm, bf16[2,256,512]{2,1,0:T(8,128)(2,1)} %constant.7.clone.zf_hbm, bf16[2,256,512]{2,1,0:T(8,128)(2,1)} %constant.8.clone.zi_hbm), custom_call_target="tpu_custom_call" | custom-call | tf_op jit(solution)/shard_map/poisson/pallas_call | solution.py:350
  80.0 2.3 %copy.7 = f32[64,64,32]{1,2,0:T(8,128)} copy(f32[64,64,32]{1,2,0:T(8,128)} %bitcast.2) | data formatting | bytes 1048576

commit v2 on v1

--- a/solution.py
+++ b/solution.py
@@ -79,9 +79,20 @@
     def wait_bytes(part, sem):
         pltpu.make_async_copy(part, part, sem).wait()
 
+    def hops(o):
+        ring = (0, 1, 2, 1)
+        return ring[o & 3] + 2 * ((o >> 2) & 1) + ring[(o >> 3) & 3]
+
+    far_first = sorted(range(1, GROUP), key=hops, reverse=True)
+
     def each_peer(count, body):
+        if count == GROUP:
+            for o in far_first:
+                body(lax.bitwise_xor(me, o))
+            return
+
         def step(o, carry):
-            body(lax.bitwise_xor(me, o))
+            body(lax.bitwise_xor(me, lax.rem(o * 19, count)))
             return carry
 
         lax.fori_loop(1, count, step, 0, unroll=8)
@@ -374,11 +385,12 @@
             dma, dma, dma((2,)), dma((2,)), dma((2,)), dma((2,)),
         ],
         compiler_params=pltpu.CompilerParams(
-            collective_id=1, has_side_effects=True, vmem_limit_bytes=56 * 2**20
+            collective_id=1, has_side_effects=True, vmem_limit_bytes=34 * 2**20
         ),
         name="poisson",
-    )(jnp.transpose(source, (0, 2, 1)), green,
-      jnp.asarray(lines), jnp.asarray(forward), jnp.asarray(inverse))
+    )(*[pltpu.with_memory_space_constraint(v, pltpu.HBM) for v in (
+        jnp.transpose(source, (0, 2, 1)), green,
+        jnp.asarray(lines), jnp.asarray(forward), jnp.asarray(inverse))])
     return jnp.transpose(result, (0, 2, 1))
 
 

time: 82.7 us -> 75.2 us (0.909)
  Pallas kernels: 80 us -> 74.1 us
  local copies, waits for them, and re-layouts: 2.26 us -> 0.97 us
    pallas_call x1, Pallas kernels: 80 us -> 74.1 us  [per_device(): pl.pallas_call(kernel, out_shape=jax.ShapeDtypeStruct((64, 32, 64), F32),...]
    unnamed x1, local copies, waits for them, and re-layouts: 2.26 us -> 0.97 us
where the time goes in v2:
time: 75.2 us; the launch traced here: 75.1 us
  Pallas kernels  74.1 us (99%)
  local copies, waits for them, and re-layouts  0.97 us (1%)
    pallas_call x1, Pallas kernels, per_device(): pl.pallas_call(kernel, out_shape=jax.ShapeDtypeStruct((64, 32, 64), F32),...  74.1 us

profile of v2, /device:TPU:0, one launch (start us, length us, event | category | flops | bytes accessed | tf_op | source)
XLA Modules:
  0.0 75.1 jit_solution(17879946662774334155)
XLA Ops:
  0.0 74.1 %poisson.1 = f32[64,32,64]{2,1,0:T(8,128)S(1)} custom-call(f32[64,32,64]{2,1,0:T(8,128)} %bitcast.3, f32[512,16,128]{2,1,0:T(8,128)} %green_hbm.1, bf16[6,256,256]{2,1,0:T(8,128)(2,1)} %constant.6.clone.lines_hbm, bf16[2,256,512]{2,1,0:T(8,128)(2,1)} %constant.7.clone.zf_hbm, bf16[2,256,512]{2,1,0:T(8,128)(2,1)} %constant.8.clone.zi_hbm), custom_call_target="tpu_custom_call" | custom-call | tf_op jit(solution)/shard_map/poisson/pallas_call | solution.py:361
  74.1 1.0 %copy.7 = f32[64,64,32]{1,2,0:T(8,128)} copy(f32[64,64,32]{1,2,0:T(8,128)S(1)} %bitcast.2) | data formatting | bytes 1048576

commit v3 on v2

--- a/solution.py
+++ b/solution.py
@@ -179,7 +179,7 @@
                 zs[pl.ds(row + 16, 16), th * 128:(th + 1) * 128] = jnp.where(low_lane, half_turn(left), right)
             return carry
 
-        lax.fori_loop(0, GZ, gather, 0, unroll=2)
+        lax.fori_loop(0, GZ, gather, 0, unroll=True)
         zb[...] = dot3(split(jnp.transpose(zs[...])), (zf[0], zf[1]))
 
         def forward_y(t, carry):
@@ -200,7 +200,7 @@
                 snd_view[1, i, :, 2 * t + h] = minus.reshape(GX, GZ, 8, 128)
             return carry
 
-        lax.fori_loop(0, GY // 2, forward_y, 0)
+        lax.fori_loop(0, GY // 2, forward_y, 0, unroll=True)
         send2(0, i)
     for i in range(2):
         send2(1, i)
@@ -311,7 +311,7 @@
             )
             return carry
 
-        lax.fori_loop(0, GY // 2, inverse_y, 0)
+        lax.fori_loop(0, GY // 2, inverse_y, 0, unroll=True)
         high, low = split(zb[...])
         zs[...] = (dot_t(zi[0], high) + (dot_t(zi[1], high) + dot_t(zi[0], low))) * (1.0 / 134217728.0)
 
@@ -324,7 +324,7 @@
                 snd4[i, (2 * th + 1) * GZ + t] = jnp.where(low_lane, half_turn(upper), lower)
             return carry
 
-        lax.fori_loop(0, GZ, scatter, 0, unroll=2)
+        lax.fori_loop(0, GZ, scatter, 0, unroll=True)
 
         def send4(peer):
             pltpu.make_async_remote_copy(

time: 75.2 us -> 74 us (0.984)
  Pallas kernels: 74.1 us -> 72.9 us
    pallas_call x1, Pallas kernels: 74.1 us -> 72.9 us  [per_device(): pl.pallas_call(kernel, out_shape=jax.ShapeDtypeStruct((64, 32, 64), F32),...]
where the time goes in v3:
time: 74 us; the launch traced here: 73.9 us
  Pallas kernels  72.9 us (99%)
  local copies, waits for them, and re-layouts  0.97 us (1%)
    pallas_call x1, Pallas kernels, per_device(): pl.pallas_call(kernel, out_shape=jax.ShapeDtypeStruct((64, 32, 64), F32),...  72.9 us

profile of v3, /device:TPU:0, one launch (start us, length us, event | category | flops | bytes accessed | tf_op | source)
XLA Modules:
  0.0 73.9 jit_solution(7614108021834835365)
XLA Ops:
  0.0 72.9 %poisson.1 = f32[64,32,64]{2,1,0:T(8,128)S(1)} custom-call(f32[64,32,64]{2,1,0:T(8,128)} %bitcast.3, f32[512,16,128]{2,1,0:T(8,128)} %green_hbm.1, bf16[6,256,256]{2,1,0:T(8,128)(2,1)} %constant.6.clone.lines_hbm, bf16[2,256,512]{2,1,0:T(8,128)(2,1)} %constant.7.clone.zf_hbm, bf16[2,256,512]{2,1,0:T(8,128)(2,1)} %constant.8.clone.zi_hbm), custom_call_target="tpu_custom_call" | custom-call | tf_op jit(solution)/shard_map/poisson/pallas_call | solution.py:361
  72.9 1.0 %copy.7 = f32[64,64,32]{1,2,0:T(8,128)} copy(f32[64,64,32]{1,2,0:T(8,128)S(1)} %bitcast.2) | data formatting | bytes 1048576

commit v4 on v3

--- a/solution.py
+++ b/solution.py
@@ -68,8 +68,9 @@
     q = b * GZ + c
     me = a * GROUP + q
 
-    load_src = pltpu.make_async_copy(src_hbm, src, in_sem)
-    load_src.start()
+    load_src = [pltpu.make_async_copy(src_hbm.at[:, i], src.at[i], in_sem.at[i]) for i in range(2)]
+    for load in load_src:
+        load.start()
     loads = [pltpu.make_async_copy(lines_hbm, lines, tab_sem.at[0]),
              pltpu.make_async_copy(zf_hbm, zf, tab_sem.at[1]),
              pltpu.make_async_copy(zi_hbm, zi, tab_sem.at[2])]
@@ -105,15 +106,18 @@
     each_peer(GROUP, greet)
     for o in range(1, GX):
         greet(lax.bitwise_xor(me, o * GROUP))
-    load_src.wait()
-
-    def pack_x(p, carry):
-        for i in range(2):
-            plane = src[2 * p + i]
+
+    def pack_plane(i):
+        load_src[i].wait()
+
+        def pack_x(p, carry):
+            plane = src[i, p]
             pack[i, p] = wide(plane[:16], plane[16:])
-        return carry
-
-    lax.fori_loop(0, GROUP, pack_x, 0, unroll=4)
+            return carry
+
+        lax.fori_loop(0, GROUP, pack_x, 0, unroll=8)
+
+    pack_plane(0)
     pl.semaphore_wait(bar, GROUP - 1 + GX - 1)
 
     for i in range(2):
@@ -125,6 +129,8 @@
 
         each_peer(GROUP, send1)
         got1[i, q] = pack[i, q]
+        if i == 0:
+            pack_plane(1)
 
     pltpu.make_async_copy(green_hbm.at[pl.ds(0, 257)], gbuf.at[pl.ds(0, 257)], green_sem).start()
 
@@ -364,7 +370,7 @@
         in_specs=[pl.BlockSpec(memory_space=pl.ANY)] * 5,
         out_specs=pl.BlockSpec(memory_space=vmem),
         scratch_shapes=[
-            vmem((64, 32, 64), F32),
+            vmem((2, GROUP, 32, 64), F32),
             vmem((2, GROUP, 16, 128), F32),
             vmem((6, 256, 256), BF16),
             vmem((2, 256, 512), BF16),
@@ -381,7 +387,7 @@
             vmem((2, 512, 128), F32),
             vmem((2, GROUP, 16, 128), F32),
             vmem((2, GROUP, 16, 128), F32),
-            dma, dma((3,)), dma, dma((2,)), dma((2,)), dma((2,)), dma((2,)),
+            dma((2,)), dma((3,)), dma, dma((2,)), dma((2,)), dma((2,)), dma((2,)),
             dma, dma, dma((2,)), dma((2,)), dma((2,)), dma((2,)),
         ],
         compiler_params=pltpu.CompilerParams(
@@ -389,7 +395,7 @@
         ),
         name="poisson",
     )(*[pltpu.with_memory_space_constraint(v, pltpu.HBM) for v in (
-        jnp.transpose(source, (0, 2, 1)), green,
+        jnp.transpose(source, (0, 2, 1)).reshape(GROUP, 2, 32, 64), green,
         jnp.asarray(lines), jnp.asarray(forward), jnp.asarray(inverse))])
     return jnp.transpose(result, (0, 2, 1))
 

time: 74 us -> 74 us (level)
  no operation moved by 1% of the time
where the time goes in v4:
time: 74 us; the launch traced here: 73.9 us
  Pallas kernels  72.9 us (99%)
  local copies, waits for them, and re-layouts  0.97 us (1%)
    pallas_call x1, Pallas kernels, per_device(): pl.pallas_call(kernel, out_shape=jax.ShapeDtypeStruct((64, 32, 64), F32),...  72.9 us

profile of v4, /device:TPU:0, one launch (start us, length us, event | category | flops | bytes accessed | tf_op | source)
XLA Modules:
  0.0 73.9 jit_solution(16315427294185920311)
XLA Ops:
  0.0 72.9 %poisson.1 = f32[64,32,64]{2,1,0:T(8,128)S(1)} custom-call(f32[32,2,32,64]{3,2,1,0:T(8,128)} %bitcast.5, f32[512,16,128]{2,1,0:T(8,128)} %green_hbm.1, bf16[6,256,256]{2,1,0:T(8,128)(2,1)} %constant.6.clone.lines_hbm, bf16[2,256,512]{2,1,0:T(8,128)(2,1)} %constant.7.clone.zf_hbm, bf16[2,256,512]{2,1,0:T(8,128)(2,1)} %constant.8.clone.zi_hbm), custom_call_target="tpu_custom_call" | custom-call | tf_op jit(solution)/shard_map/poisson/pallas_call | solution.py:367
  72.9 1.0 %copy.7 = f32[64,64,32]{1,2,0:T(8,128)} copy(f32[64,64,32]{1,2,0:T(8,128)S(1)} %bitcast.4) | data formatting | bytes 1048576

commit v5 on v4

--- a/solution.py
+++ b/solution.py
@@ -86,14 +86,14 @@
 
     far_first = sorted(range(1, GROUP), key=hops, reverse=True)
 
-    def each_peer(count, body):
+    def each_peer(count, body, factor=19):
         if count == GROUP:
             for o in far_first:
                 body(lax.bitwise_xor(me, o))
             return
 
         def step(o, carry):
-            body(lax.bitwise_xor(me, lax.rem(o * 19, count)))
+            body(lax.bitwise_xor(me, lax.rem(o * factor, count)))
             return carry
 
         lax.fori_loop(1, count, step, 0, unroll=8)
@@ -279,7 +279,7 @@
                     device_id=peer, device_id_type=FLAT
                 ).start()
 
-            each_peer(ALL, send30)
+            each_peer(ALL, send30, 83)
             back0[me] = rcv[0, pl.ds(2 * me, 2)]
         else:
             for i in range(2):
@@ -289,7 +289,7 @@
                         device_id=peer, device_id_type=FLAT
                     ).start()
 
-                each_peer(ALL, send31)
+                each_peer(ALL, send31, 83)
                 back1[i, me] = rcv[1, 2 * me + i]
 
     back0_view = back0.reshape(GX, GY, GZ, 2, 8, 128)

time: 74 us -> 74 us (level)
  no operation moved by 1% of the time
where the time goes in v5:
time: 74 us; the launch traced here: 73.8 us
  Pallas kernels  72.9 us (99%)
  local copies, waits for them, and re-layouts  0.97 us (1%)
    pallas_call x1, Pallas kernels, per_device(): pl.pallas_call(kernel, out_shape=jax.ShapeDtypeStruct((64, 32, 64), F32),...  72.9 us

profile of v5, /device:TPU:0, one launch (start us, length us, event | category | flops | bytes accessed | tf_op | source)
XLA Modules:
  0.0 73.8 jit_solution(16052852970970492341)
XLA Ops:
  0.0 72.9 %poisson.1 = f32[64,32,64]{2,1,0:T(8,128)S(1)} custom-call(f32[32,2,32,64]{3,2,1,0:T(8,128)} %bitcast.5, f32[512,16,128]{2,1,0:T(8,128)} %green_hbm.1, bf16[6,256,256]{2,1,0:T(8,128)(2,1)} %constant.6.clone.lines_hbm, bf16[2,256,512]{2,1,0:T(8,128)(2,1)} %constant.7.clone.zf_hbm, bf16[2,256,512]{2,1,0:T(8,128)(2,1)} %constant.8.clone.zi_hbm), custom_call_target="tpu_custom_call" | custom-call | tf_op jit(solution)/shard_map/poisson/pallas_call | solution.py:367
  72.9 1.0 %copy.7 = f32[64,64,32]{1,2,0:T(8,128)} copy(f32[64,64,32]{1,2,0:T(8,128)S(1)} %bitcast.4) | data formatting | bytes 1048576
